TPU v7x, 32 devices: a 4x4x1 block of a 4x4x8 slice. The times are simulated.
32 devices in a mesh: rep: 1 (over z), r: 4 (over y), s: 8 (over x, core).
Axes of the slice: x: 4, y: 4, z: 1, core: 2. Of those that a mesh axis runs over, the one named last changes fastest.
The devices are a block of a 4x4x8 slice.
Arguments:
- x: bfloat16 [32, 2048, 1024], P(('rep', 'r', 's'))
- dy: bfloat16 [32, 2048, 1024], P(('rep', 'r', 's'))
- w_gate: bfloat16 [2, 1024, 3200], P(None, 's')
- w_up: bfloat16 [2, 1024, 3200], P(None, 's')
- w_down: bfloat16 [2, 3200, 1024], P(None, 's')
- m_w_gate: float32 [2, 1024, 3200], P(None, 's')
- m_w_up: float32 [2, 1024, 3200], P(None, 's')
- m_w_down: float32 [2, 3200, 1024], P(None, 's')
- v_w_gate: float32 [2, 1024, 3200], P(None, 's')
- v_w_up: float32 [2, 1024, 3200], P(None, 's')
- v_w_down: float32 [2, 3200, 1024], P(None, 's')
Outputs:
- output 1: bfloat16 [2, 1024, 3200], P('rep', 's')
- output 2: bfloat16 [2, 1024, 3200], P('rep', 's')
- output 3: bfloat16 [2, 3200, 1024], P('rep', 's')
- output 4: float32 [2, 1024, 3200], P('rep', 's')
- output 5: float32 [2, 1024, 3200], P('rep', 's')
- output 6: float32 [2, 3200, 1024], P('rep', 's')
- output 7: float32 [2, 1024, 3200], P('rep', 's')
- output 8: float32 [2, 1024, 3200], P('rep', 's')
- output 9: float32 [2, 3200, 1024], P('rep', 's')
All inputs are finite; a program needn't handle non-finite values.
Results may differ from a plain program's by a relative error of at most 0.022.
Values are sent between devices in bfloat16 or wider.
A program may use at most 768 MiB of HBM per device.

v0:
```python
import jax
import jax.numpy as jnp
from jax import lax
from jax.sharding import PartitionSpec as P

NAMES = ("w_gate", "w_up", "w_down")


def matmul(a, w):
    return jnp.dot(a, w, preferred_element_type=jnp.float32).astype(jnp.bfloat16)


def normed(h):
    wide = h.astype(jnp.float32)
    scale = lax.rsqrt(jnp.mean(wide**2, -1, keepdims=True) + 1e-6)
    return (wide * scale).astype(jnp.bfloat16)


def layer(h, w):
    a = normed(h)
    gate = jnp.dot(a, w["w_gate"], preferred_element_type=jnp.float32)
    up = jnp.dot(a, w["w_up"], preferred_element_type=jnp.float32)
    return h + matmul((jax.nn.silu(gate) * up).astype(jnp.bfloat16), w["w_down"])


def adamw(w, m, v, g):
    m = 0.9 * m + 0.1 * g
    v = 0.95 * v + 0.05 * g * g
    step = m * lax.rsqrt(v + 1e-8) + 0.1 * w
    return (w - 0.02 * step).astype(jnp.bfloat16), m, v


def clipped(gradients, sum_of_squares, count):
    factor = jnp.minimum(1.0, 0.5 * lax.rsqrt(sum_of_squares / count + 1e-30))
    return [g * factor for g in gradients]


def solution(mesh):
    def fetched(weights, number):
        return {name: lax.all_gather(w[number], "s", axis=0, tiled=True) for name, w in zip(NAMES, weights, strict=True)}

    def summed(term):
        return lax.psum(lax.psum_scatter(term, "s", scatter_dimension=0, tiled=True), "r")

    def step(x, dy, *arrays):
        weights, m, v = (arrays[i : i + 3] for i in (0, 3, 6))
        layers = weights[0].shape[0]
        h, kept = x[0], []
        for number in range(layers):
            kept.append(h)
            h = layer(h, fetched(weights, number))
        by_h, mine = dy[0], [None] * layers
        for number in reversed(range(layers)):
            _, back = jax.vjp(lambda w, h: layer(h, w), fetched(weights, number), kept[number])
            by_w, by_h = back(by_h)
            mine[number] = [summed(by_w[name]) for name in NAMES]
        gradients = [jnp.stack([mine[number][i] for number in range(layers)]).astype(jnp.float32) for i in range(3)]
        squares = lax.psum(sum(jnp.sum(g * g) for g in gradients), "s")
        gradients = clipped(gradients, squares, lax.psum(1, "s") * sum(g.size for g in gradients))
        new = [adamw(w.astype(jnp.float32), m, v, g) for w, m, v, g in zip(weights, m, v, gradients, strict=True)]
        return tuple(one[which] for which in range(3) for one in new)

    states, cut = P(("rep", "r", "s"), None, None), P(None, "s", None)
    return jax.shard_map(
        step,
        mesh=mesh,
        in_specs=(states, states) + (cut,) * 9,
        out_specs=(P("rep", "s", None),) * 9,
        check_vma=False,
    )
```

profile of v0, /device:TPU:96, one launch (start us, length us, event | category | flops | bytes accessed | tf_op | source)
XLA Modules:
  0.0 781.4 jit_solution(8689882602759051022)
XLA Ops:
  32.5 19.5 %all-gather.13.cloned.1.call-done = bf16[1,1024,3200]{2,1,0:T(8,128)(2,1)} async-done(((bf16[1,128,3200]{2,1,0:T(8,128)(2,1)}), bf16[1,1024,3200]{2,1,0:T(8,128)(2,1)}) %all-gather.13.cloned.1.call-update) | async-done | bytes 6553616 | tf_op jit(solution)/shard_map/all_gather | solution.py:40
  52.0 22.9 %fusion.41 = f32[2048,3200]{1,0:T(8,128)} fusion(bf16[1,1024,3200]{2,1,0:T(8,128)(2,1)} %all-gather.13.cloned.1.call-done, bf16[1,2048,1024]{1,2,0:T(8,128)(2,1)} %copy.20, f32[2048]{0:T(1024)S(1)} %add_rsqrt_fusion), kind=kOutput, calls=%fused_computation.59 | convolution fusion | flops 13428064256 | bytes 36970496 | tf_op jit(solution)/shard_map/dot_general | solution.py:21
  74.9 18.6 %all-gather.15.cloned.1.call-done = bf16[1,1024,3200]{2,1,0:T(8,128)(2,1)} async-done(((bf16[1,128,3200]{2,1,0:T(8,128)(2,1)}), bf16[1,1024,3200]{2,1,0:T(8,128)(2,1)}) %all-gather.15.cloned.1.call-update) | async-done | bytes 6553616 | tf_op jit(solution)/shard_map/all_gather | solution.py:40
  93.5 31.4 %multiply_convert_fusion.1 = (bf16[2048,3200]{1,0:T(8,128)(2,1)}, f32[2048,3200]{1,0:T(8,128)}) fusion(f32[2048,3200]{1,0:T(8,128)} %fusion.41, bf16[1,1024,3200]{2,1,0:T(8,128)(2,1)} %all-gather.15.cloned.1.call-done, bf16[1,2048,1024]{1,2,0:T(8,128)(2,1)} %copy.20, f32[2048]{0:T(1024)S(1)} %add_rsqrt_fusion), kind=kOutput, calls=%fused_computation.17 | convolution fusion | flops 13467385856 | bytes 76292096 | tf_op jit(solution)/shard_map/dot_general | solution.py:22
  135.0 21.8 %fusion.19 = (f32[2048]{0:T(1024)S(1)}, bf16[2048,1024]{0,1:T(8,128)(2,1)}) fusion(bf16[2048,3200]{1,0:T(8,128)(2,1)} %get-tuple-element.30, bf16[1,3200,1024]{2,1,0:T(8,128)(2,1)} %all-gather.17.cloned.1.call-done, bf16[1,2048,1024]{1,2,0:T(8,128)(2,1)} %copy.20), kind=kOutput, calls=%fused_computation.37 | convolution fusion | flops 13432256512 | bytes 28057600 | tf_op jit(solution)/shard_map/dot_general | solution.py:10
  156.8 19.5 %all-gather.21.cloned.1.call-done = bf16[1,3200,1024]{2,1,0:T(8,128)(2,1)} async-done(((bf16[1,400,1024]{2,1,0:T(8,128)(2,1)}), bf16[1,3200,1024]{2,1,0:T(8,128)(2,1)}) %all-gather.21.cloned.1.call-update) | async-done | bytes 6553616 | tf_op jit(solution)/shard_map/all_gather | solution.py:40
  176.4 20.9 %convolution_convert_fusion.1 = bf16[2048,3200]{1,0:T(8,128)(2,1)} fusion(bf16[1,3200,1024]{2,1,0:T(8,128)(2,1)} %all-gather.21.cloned.1.call-done, bf16[1,2048,1024]{2,1,0:T(8,128)(2,1)} %param.12), kind=kOutput, calls=%fused_computation.23 | convolution fusion | flops 13428326400 | bytes 23855104 | tf_op jit(solution)/shard_map/transpose(jvp())/dot_general | solution.py:10
  197.3 20.4 %all-gather.23.cloned.1.call-done = bf16[1,1024,3200]{2,1,0:T(8,128)(2,1)} async-done(((bf16[1,128,3200]{2,1,0:T(8,128)(2,1)}), bf16[1,1024,3200]{2,1,0:T(8,128)(2,1)}) %all-gather.23.cloned.1.call-update) | async-done | bytes 6553616 | tf_op jit(solution)/shard_map/all_gather | solution.py:40
  217.7 22.8 %fusion.28 = f32[2048,3200]{1,0:T(8,128)} fusion(bf16[1,1024,3200]{2,1,0:T(8,128)(2,1)} %all-gather.23.cloned.1.call-done, bf16[2048,1024]{0,1:T(8,128)(2,1)} %get-tuple-element.33, f32[2048]{0:T(1024)S(1)} %fusion.80), kind=kOutput, calls=%fused_computation.46 | convolution fusion | flops 13428064256 | bytes 36970496 | tf_op jit(solution)/shard_map/jvp()/dot_general | solution.py:22
  240.5 18.6 %all-gather.19.cloned.1.call-done = bf16[1,1024,3200]{2,1,0:T(8,128)(2,1)} async-done(((bf16[1,128,3200]{2,1,0:T(8,128)(2,1)}), bf16[1,1024,3200]{2,1,0:T(8,128)(2,1)}) %all-gather.19.cloned.1.call-update) | async-done | bytes 6553616 | tf_op jit(solution)/shard_map/all_gather | solution.py:40
  259.1 38.7 %fusion.2 = (bf16[2048,3200]{1,0:T(8,128)(2,1)}, f32[2048,3200]{1,0:T(8,128)}) fusion(f32[2048,3200]{1,0:T(8,128)} %fusion.28, bf16[2048,3200]{1,0:T(8,128)(2,1)} %convolution_convert_fusion.1, bf16[1,1024,3200]{2,1,0:T(8,128)(2,1)} %all-gather.19.cloned.1.call-done, bf16[2048,1024]{0,1:T(8,128)(2,1)} %get-tuple-element.33, f32[2048]{0:T(1024)S(1)} %fusion.80), kind=kOutput, calls=%fused_computation.8 | convolution fusion | flops 13506707456 | bytes 89399296 | tf_op jit(solution)/shard_map/jvp()/dot_general | solution.py:21
  297.8 22.6 %fusion.12 = bf16[2048,1024]{0,1:T(8,128)(2,1)} fusion(bf16[2048,3200]{1,0:T(8,128)(2,1)} %convolution_convert_fusion.1, bf16[1,1024,3200]{2,1,0:T(8,128)(2,1)} %all-gather.23.cloned.1.call-done, f32[2048,3200]{1,0:T(8,128)} %get-tuple-element.35), kind=kOutput, calls=%fused_computation.21 | convolution fusion | flops 13461094400 | bytes 50069504 | tf_op jit(solution)/shard_map/transpose(jvp())/dot_general | solution.py:22
  320.4 21.8 %fusion.21 = (f32[2048]{0:T(1024)S(1)}, bf16[2048,1024]{0,1:T(8,128)(2,1)}) fusion(bf16[2048,1024]{0,1:T(8,128)(2,1)S(1)} %copy-done.6, bf16[2048,1024]{0,1:T(8,128)(2,1)} %fusion.12, bf16[2048,3200]{1,0:T(8,128)(2,1)} %get-tuple-element.34, bf16[1,1024,3200]{2,1,0:T(8,128)(2,1)} %all-gather.19.cloned.1.call-done), kind=kOutput, calls=%fused_computation.39 | convolution fusion | flops 13432256512 | bytes 32251904 | tf_op jit(solution)/shard_map/transpose(jvp())/dot_general | solution.py:21
  349.2 19.5 %convolution_convert_fusion.2 = bf16[3200,1024]{1,0:T(8,128)(2,1)} fusion(bf16[2048,3200]{1,0:T(8,128)(2,1)} %get-tuple-element.30, bf16[2048,1024]{0,1:T(8,128)(2,1)S(1)} %fusion.44), kind=kOutput, calls=%fused_computation.44 | convolution fusion | flops 13425049600 | bytes 23855104 | tf_op jit(solution)/shard_map/transpose(jvp())/dot_general | solution.py:10
  368.8 26.0 %fusion.25 = bf16[3200,1024]{1,0:T(8,128)(2,1)} fusion(f32[2048,3200]{1,0:T(8,128)} %fusion.28, bf16[1,2048,1024]{2,1,0:T(8,128)(2,1)} %param.12, f32[2048,3200]{1,0:T(8,128)} %get-tuple-element.35), kind=kOutput, calls=%fused_computation.41 | convolution fusion | flops 13464371200 | bytes 63176704 | tf_op jit(solution)/shard_map/transpose(jvp())/dot_general | solution.py:10
  394.9 21.4 %convolution_convert_fusion = bf16[2048,3200]{1,0:T(8,128)(2,1)} fusion(bf16[2048,1024]{0,1:T(8,128)(2,1)} %copy-done.7, bf16[1,3200,1024]{2,1,0:T(8,128)(2,1)} %all-gather.17.cloned.1.call-done), kind=kOutput, calls=%fused_computation.22 | convolution fusion | flops 13428326400 | bytes 23855104 | tf_op jit(solution)/shard_map/transpose(jvp())/dot_general | solution.py:10
  416.4 24.3 %fusion.27 = bf16[1024,3200]{1,0:T(8,128)(2,1)} fusion(bf16[2048,3200]{1,0:T(8,128)(2,1)} %convolution_convert_fusion, f32[2048,3200]{1,0:T(8,128)} %fusion.41, bf16[1,2048,1024]{1,2,0:T(8,128)(2,1)S(1)} %copy-done.1, f32[2048]{0:T(1024)S(1)} %copy-done.20), kind=kOutput, calls=%fused_computation.43 | convolution fusion | flops 13470662656 | bytes 50077696 | tf_op jit(solution)/shard_map/transpose(jvp())/dot_general | solution.py:22
  441.4 25.5 %fusion.26 = bf16[1024,3200]{1,0:T(8,128)(2,1)} fusion(bf16[2048,3200]{1,0:T(8,128)(2,1)} %convolution_convert_fusion.1, bf16[2048,1024]{0,1:T(8,128)(2,1)} %get-tuple-element.33, f32[2048]{0:T(1024)S(1)} %copy-done.16, f32[2048,3200]{1,0:T(8,128)} %get-tuple-element.35), kind=kOutput, calls=%fused_computation.42 | convolution fusion | flops 13470662656 | bytes 50077696 | tf_op jit(solution)/shard_map/transpose(jvp())/dot_general | solution.py:22
  467.0 32.6 %fusion.22 = bf16[1024,3200]{1,0:T(8,128)(2,1)} fusion(f32[2048,3200]{1,0:T(8,128)} %fusion.41, f32[2048,3200]{1,0:T(8,128)} %get-tuple-element.31, bf16[2048,3200]{1,0:T(8,128)(2,1)} %convolution_convert_fusion, bf16[1,2048,1024]{1,2,0:T(8,128)(2,1)} %copy.20, f32[2048]{0:T(1024)S(1)} %copy-done.20), kind=kOutput, calls=%fused_computation.40 | convolution fusion | flops 13503430656 | bytes 76292096 | tf_op jit(solution)/shard_map/transpose(jvp())/dot_general | solution.py:21
  499.7 21.1 %convolution_convert_fusion.3 = bf16[1024,3200]{1,0:T(8,128)(2,1)} fusion(bf16[2048,3200]{1,0:T(8,128)(2,1)} %get-tuple-element.34, bf16[2048,1024]{0,1:T(8,128)(2,1)} %get-tuple-element.33, f32[2048]{0:T(1024)S(1)} %copy-done.16), kind=kOutput, calls=%fused_computation.45 | convolution fusion | flops 13428064256 | bytes 23863296 | tf_op jit(solution)/shard_map/transpose(jvp())/dot_general | solution.py:21
  521.0 18.9 %reduce-scatter.13.cloned.1.call-done = bf16[128,3200]{1,0:T(8,128)(2,1)} async-done(((bf16[1024,3200]{1,0:T(8,128)(2,1)}), bf16[128,3200]{1,0:T(8,128)(2,1)}) %reduce-scatter.13.cloned.1.call-update) | async-done | bytes 819216 | tf_op jit(solution)/shard_map/reduce_scatter | solution.py:43
  539.9 43.3 %reduce-scatter.7.cloned.1.call-done = bf16[128,3200]{1,0:T(8,128)(2,1)} async-done(((bf16[1024,3200]{1,0:T(8,128)(2,1)}), bf16[128,3200]{1,0:T(8,128)(2,1)}) %reduce-scatter.7.cloned.1.call-update) | async-done | bytes 819216 | tf_op jit(solution)/shard_map/reduce_scatter | solution.py:43
  583.2 43.1 %reduce-scatter.9.cloned.1.call-done = bf16[128,3200]{1,0:T(8,128)(2,1)} async-done(((bf16[1024,3200]{1,0:T(8,128)(2,1)}), bf16[128,3200]{1,0:T(8,128)(2,1)}) %reduce-scatter.9.cloned.1.call-update) | async-done | bytes 819216 | tf_op jit(solution)/shard_map/reduce_scatter | solution.py:43
  626.4 101.8 %all-reduce.3.cloned.1.call-done = (bf16[1,128,3200]{2,1,0:T(8,128)(2,1)}, bf16[1,128,3200]{2,1,0:T(8,128)(2,1)}, bf16[1,128,3200]{2,1,0:T(8,128)(2,1)}, bf16[1,...) async-done(((bf16[1,128,3200]{2,1,0:T(8,128)(2,1)}, bf16[1,128,3200]{2,1,0:T(8,128)(2,1)}, bf16[1,128,3200]{2,1,0:T(8,128)(2,1)}, ...) | async-done | bytes 4915216 | tf_op jit(solution)/shard_map/psum | solution.py:43
  (88 shorter events, 87.3 us)
Async XLA Ops:
  7.2 44.8 %all-gather.13.cloned.1.call-start = ((), (), s32[]{:S(2)}) async-start(), calls=%async_computation.12 | async-start | bytes 7372800 | tf_op jit(solution)/shard_map/all_gather | solution.py:40
  10.1 83.4 %all-gather.15.cloned.1.call-start = ((), (), s32[]{:S(2)}) async-start(), calls=%async_computation.13 | async-start | bytes 7372800 | tf_op jit(solution)/shard_map/all_gather | solution.py:40
  12.9 122.1 %all-gather.17.cloned.1.call-start = ((), (), s32[]{:S(2)}) async-start(), calls=%async_computation.14 | async-start | bytes 7372800 | tf_op jit(solution)/shard_map/all_gather | solution.py:40
  14.3 162.0 %all-gather.21.cloned.1.call-start = ((), (), s32[]{:S(2)}) async-start(), calls=%async_computation.16 | async-start | bytes 7372800 | tf_op jit(solution)/shard_map/all_gather | solution.py:40
  15.0 202.8 %all-gather.23.cloned.1.call-start = ((), (), s32[]{:S(2)}) async-start(), calls=%async_computation.17 | async-start | bytes 7372800 | tf_op jit(solution)/shard_map/all_gather | solution.py:40
  15.6 243.5 %all-gather.19.cloned.1.call-start = ((), (), s32[]{:S(2)}) async-start(), calls=%async_computation.15 | async-start | bytes 7372800 | tf_op jit(solution)/shard_map/all_gather | solution.py:40
  16.3 504.7 %reduce-scatter.15.cloned.1.call-start = ((), (), s32[]{:S(2)}) async-start(), calls=%async_computation.10 | async-start | bytes 7372800 | tf_op jit(solution)/shard_map/reduce_scatter | solution.py:43
  25.9 67.6 %copy-start.19 = (f32[2048]{0:T(1024)}, f32[2048]{0:T(1024)S(1)}, u32[]{:S(2)}) copy-start(f32[2048]{0:T(1024)S(1)} %add_rsqrt_fusion) | copy-start | bytes 24580
  156.8 40.5 %copy-start.17 = (f32[2048]{0:T(1024)}, f32[2048]{0:T(1024)S(1)}, u32[]{:S(2)}) copy-start(f32[2048]{0:T(1024)S(1)} %get-tuple-element.32) | copy-start | bytes 24580
  156.8 185.4 %copy-start.15 = (f32[2048]{0:T(1024)}, f32[2048]{0:T(1024)S(1)}, u32[]{:S(2)}) copy-start(f32[2048]{0:T(1024)S(1)} %fusion.80) | copy-start | bytes 24580
  297.8 22.6 %copy-start.6 = (bf16[2048,1024]{0,1:T(8,128)(2,1)S(1)}, bf16[2048,1024]{0,1:T(8,128)(2,1)}, u32[]{:S(2)}) copy-start(bf16[2048,1024]{0,1:T(8,128)(2,1)} %get-tuple-element.33) | copy-start | bytes 12582916
  320.4 21.9 %copy-start.18 = (f32[2048]{0:T(1024)S(1)}, f32[2048]{0:T(1024)}, u32[]{:S(2)}) copy-start(f32[2048]{0:T(1024)} %copy-done.17) | copy-start | bytes 24580
  320.4 21.9 %copy-start = (bf16[1,2048,1024]{1,2,0:T(8,128)(2,1)S(1)}, bf16[1,2048,1024]{1,2,0:T(8,128)(2,1)}, u32[]{:S(2)}) copy-start(bf16[1,2048,1024]{1,2,0:T(8,128)(2,1)} %copy.21) | copy-start | bytes 12582916
  368.7 152.2 %reduce-scatter.17.cloned.1.call-start = ((), (), s32[]{:S(2)}) async-start(), calls=%async_computation.11 | async-start | bytes 7372800 | tf_op jit(solution)/shard_map/reduce_scatter | solution.py:43
  394.9 21.5 %copy-start.20 = (f32[2048]{0:T(1024)S(1)}, f32[2048]{0:T(1024)}, u32[]{:S(2)}) copy-start(f32[2048]{0:T(1024)} %copy-done.19) | copy-start | bytes 24580
  394.9 126.1 %reduce-scatter.11.cloned.1.call-start = ((), (), s32[]{:S(2)}) async-start(), calls=%async_computation.8 | async-start | bytes 7372800 | tf_op jit(solution)/shard_map/reduce_scatter | solution.py:43
  394.9 21.5 %copy-start.1 = (bf16[1,2048,1024]{1,2,0:T(8,128)(2,1)S(1)}, bf16[1,2048,1024]{1,2,0:T(8,128)(2,1)}, u32[]{:S(2)}) copy-start(bf16[1,2048,1024]{1,2,0:T(8,128)(2,1)} %copy.20) | copy-start | bytes 12582916
  440.8 99.1 %reduce-scatter.13.cloned.1.call-start = ((), (), s32[]{:S(2)}) async-start(), calls=%async_computation.9 | async-start | bytes 7372800 | tf_op jit(solution)/shard_map/reduce_scatter | solution.py:43
  466.9 116.2 %reduce-scatter.7.cloned.1.call-start = ((), (), s32[]{:S(2)}) async-start(), calls=%async_computation.6 | async-start | bytes 7372800 | tf_op jit(solution)/shard_map/reduce_scatter | solution.py:43
  499.6 126.7 %reduce-scatter.9.cloned.1.call-start = ((), (), s32[]{:S(2)}) async-start(), calls=%async_computation.7 | async-start | bytes 7372800 | tf_op jit(solution)/shard_map/reduce_scatter | solution.py:43
  520.8 233.6 %copy-start.3 = (bf16[2,400,1024]{2,1,0:T(8,128)(2,1)S(1)}, bf16[2,400,1024]{2,1,0:T(8,128)(2,1)}, u32[]{:S(2)}) copy-start(bf16[2,400,1024]{2,1,0:T(8,128)(2,1)} %param.15) | copy-start | bytes 4915204
  520.8 207.3 %all-reduce.3.cloned.1.call-start = ((), (), s32[]{:S(2)}) async-start(), calls=%async_computation.18 | async-start | bytes 9830400 | tf_op jit(solution)/shard_map/psum | solution.py:43
  754.5 10.1 %copy-start.13 = (f32[2,128,3200]{2,1,0:T(8,128)S(1)}, f32[2,128,3200]{2,1,0:T(8,128)}, u32[]{:S(2)}) copy-start(f32[2,128,3200]{2,1,0:T(8,128)} %param.16) | copy-start | bytes 9830404
  754.5 11.0 %copy-start.14 = (f32[2,128,3200]{2,1,0:T(8,128)S(1)}, f32[2,128,3200]{2,1,0:T(8,128)}, u32[]{:S(2)}) copy-start(f32[2,128,3200]{2,1,0:T(8,128)} %param.20) | copy-start | bytes 9830404
  (10 other events, 62.7 us)
Sparse Core Ops, SparseCore 0:
  10.2 41.6 all-gather.12
  54.1 39.3 all-gather.14
  95.6 39.3 all-gather.16
  137.0 39.3 all-gather.20
  178.4 39.3 all-gather.22
  219.8 39.3 all-gather.18
  368.9 41.3 reduce-scatter.14
  412.6 40.8 reduce-scatter.16
  455.9 40.8 reduce-scatter.10
  499.0 40.8 reduce-scatter.12
  542.2 40.8 reduce-scatter.6
  585.4 40.8 reduce-scatter.8
  629.1 99.0 all-reduce.2
where the time goes:
time: 789 us; the launch traced here: 781 us
  matrix products  373 us (47%)
  waiting for transfers between devices  316 us (40%)
  other arithmetic  33 us (4%)
  local copies, waits for them, and re-layouts  26 us (3%)
  between operations  17.1 us (2%)
  blocking collectives  15.1 us (2%)
    dot_general x5, matrix products, layer(): gate = jnp.dot(a, w['w_gate'], preferred_element_type=jnp.float32)  137 us
    dot_general x5, matrix products, layer(): up = jnp.dot(a, w['w_up'], preferred_element_type=jnp.float32)  127 us
    dot_general x5, matrix products, matmul(): jnp.dot(a, w, preferred_element_type=jnp.float32).astype(jnp.bfloat16)  110 us
    all_gather x6, waiting for transfers between devices, fetched(): lax.all_gather(w[number], 's', axis=0, tiled=True)  107 us
    reduce_scatter x6, waiting for transfers between devices, summed(): lax.psum_scatter(term, 's', scatter_dimension=0, tiled=True)  105 us
    psum x1, waiting for transfers between devices, summed(): lax.psum(lax.psum_scatter(term, 's', scatter_dimension=0, tiled=True), 'r')  102 us
    unnamed x44, local copies, waits for them, and re-layouts  19.3 us
    convert_element_type x2, other arithmetic, adamw(): return ((w - 0.02 * step).astype(jnp.bfloat16), m, v)  16.5 us
  transfers between devices with their start and end apart: 13, of which 10 were waited for; matrix products, arithmetic and copies ran while one was open for 37% of the time, Pallas kernels for 0%

commit v1 on v0

v1 whole, which is shorter than its diff:
```python
import functools
import itertools

import jax
import jax.numpy as jnp
from jax import lax
from jax.experimental import pallas as pl
from jax.experimental.pallas import tpu as pltpu
from jax.sharding import PartitionSpec as P

MESH = pl.DeviceIdType.MESH
BF, F32 = jnp.bfloat16, jnp.float32
ANY = pl.BlockSpec(memory_space=pl.ANY)
NT, TN = (((1,), (1,)), ((), ())), (((0,), (0,)), ((), ()))
ROWS = 16


def dot(a, b, dims=None):
    if dims is None:
        return jnp.dot(a, b, preferred_element_type=F32)
    return lax.dot_general(a, b, dims, preferred_element_type=F32)


def like(shape, dtype=BF):
    return jax.ShapeDtypeStruct(shape, dtype)


def halves(rows):
    first = -(-rows // (2 * ROWS)) * ROWS
    return (0, first), (first, rows - first)


class Place:
    def __init__(self, ns, nr):
        s, y = lax.axis_index("s"), lax.axis_index("r")
        self.ns, self.nx, self.nr, self.s = ns, ns // 2, nr, s
        self.x, self.c, self.y = lax.div(s, 2), lax.rem(s, 2), y

    def block(self, offset, other=False):
        core = 1 - self.c if other else self.c
        return 2 * lax.rem(self.x + offset, self.nx) + core

    def to(self, name):
        if name == "partner":
            return {"s": self.block(0, True)}
        if name == "x+":
            return {"s": self.block(1)}
        if name == "x-":
            return {"s": self.block(self.nx - 1)}
        if name == "y+":
            return {"r": lax.rem(self.y + 1, self.nr)}
        if name == "y-":
            return {"r": lax.rem(self.y + self.nr - 1, self.nr)}
        return {"s": lax.rem(self.s + name, self.ns)}


def rows_of(block, rows, start=0, size=None):
    return pl.ds(pl.multiple_of(block * rows + start, ROWS), rows if size is None else size)


def add(out, terms, size, squares=None):
    rows, cols = size

    def window(where, i):
        ref, row, col = where
        return ref, (pl.ds(pl.multiple_of(i * ROWS + row, ROWS), ROWS), pl.ds(pl.multiple_of(col, 128), cols))

    def one(i, _):
        total = None
        for where in terms:
            ref, at = window(where, i)
            term = ref[at].astype(F32)
            total = term if total is None else total + term
        ref, at = window(out, i)
        ref[at] = total.astype(ref.dtype)
        return 0

    lax.fori_loop(0, rows // ROWS, one, 0)


class Comm:
    late = False

    def scratch(self):
        return self.buffers() + [
            pltpu.SemaphoreType.DMA((self.remote,)),
            pltpu.SemaphoreType.DMA((self.remote,)),
            pltpu.SemaphoreType.DMA((self.local,)),
        ]

    def bind(self, place, ins, outs, scratch):
        self.p, self.i, self.o = place, ins, outs
        self.b, (self.send, self.recv, self.here) = scratch[:-3], scratch[-3:]

    def far(self, k, src, dst, to):
        return pltpu.make_async_remote_copy(
            src_ref=src, dst_ref=dst, send_sem=self.send.at[k], recv_sem=self.recv.at[k],
            device_id=self.p.to(to), device_id_type=MESH,
        )

    def near(self, k, src, dst):
        return pltpu.make_async_copy(src, dst, self.here.at[k])


class Gather(Comm):
    remote, local = 9, 2
    peers = ("partner", "x+", "x-")

    def __init__(self, w, layer, ns):
        self.layer, self.ns = layer, ns
        self.rows, self.cols = w.shape[1:]
        self.ins, self.outs = [w], [like((ns * self.rows, self.cols))]

    def buffers(self):
        return [pltpu.VMEM((self.rows, self.cols), BF)]

    def copy(self, k):
        p, out, r = self.p, self.o[0], self.rows
        own = self.i[0].at[self.layer]
        if k < 3:
            return self.far(k, own, out.at[rows_of(p.block(0), r)], ("x+", "x-", "partner")[k])
        left, right, far = p.nx - 1, 1, 2
        offset = (left, right, left, right, far, far)[k - 3]
        part = None if k in (5, 6) else (k - 3) % 2
        start, size = (0, r) if part is None else halves(r)[part]
        where = out.at[rows_of(p.block(offset), r, start, size)]
        return self.far(k, where, where, self.peers[k - 2] if k < 5 else "partner")

    def start(self):
        for k in range(3):
            self.copy(k).start()
        self.near(0, self.i[0].at[self.layer], self.b[0]).start()

    def put(self):
        return self.near(1, self.b[0], self.o[0].at[rows_of(self.p.block(0), self.rows)])

    def e0(self):
        self.near(0, self.i[0].at[self.layer], self.b[0]).wait()
        self.put().start()
        self.copy(0).wait_recv()
        self.copy(3).start()
        self.copy(5).start()
        self.copy(1).wait_recv()
        self.copy(4).start()
        self.copy(6).start()

    def e1(self):
        for k in (3, 4):
            self.copy(k).wait_recv()
            self.copy(k + 4).start()

    def e2(self):
        for k in (2, *range(5, 9)):
            self.copy(k).wait_recv()
        for k in range(9):
            self.copy(k).wait_send()
        self.put().wait()

    def events(self):
        return [self.e0, self.e1, self.e2]


class GatherAcross(Comm):
    remote, local = 29, 2
    peers = ("partner", "x+", "x-", "y+", "y-")

    def __init__(self, w, layer, ns, nr):
        self.layer, self.part = layer, w.shape[1] // nr
        self.rows, self.cols = w.shape[1:]
        self.ins, self.outs = [w], [like((ns * self.rows, self.cols))]

    def buffers(self):
        return [pltpu.VMEM((self.rows, self.cols), BF)]

    def at(self, chip, group, half=None):
        p, q = self.p, self.part
        start = lax.rem(p.y + group, p.nr) * q
        size = q if half is None else q // 2
        return self.o[0].at[rows_of(p.block(chip), self.rows, start + (0 if half is None else half * size), size)]

    def copy(self, k):
        p, q = self.p, self.part
        own = self.i[0].at[self.layer]
        left, right, far = p.nx - 1, 1, 2
        if k == 0:
            return self.far(k, own, self.o[0].at[rows_of(p.block(0), self.rows)], "partner")
        if k < 3:
            return self.far(k, own.at[rows_of(p.y, q)], self.at(0, 0), ("x+", "x-")[k - 1])
        if k < 5:
            where = self.at((left, right)[k - 3], 0, k - 3)
            return self.far(k, where, where, ("x+", "x-")[k - 3])
        which, k1 = divmod(k - 5, 8)
        chip = (left, right, far)[which]
        if k1 < 2:
            where, to = self.at(chip, 0), ("y+", "y-")[k1]
        elif k1 < 4:
            where, to = self.at(chip, (p.nr - 1, 1)[k1 - 2], k1 - 2), ("y+", "y-")[k1 - 2]
        else:
            where, to = self.at(chip, (0, p.nr - 1, 1, 2)[k1 - 4]), "partner"
        return self.far(k, where, where, to)

    def start(self):
        for k in (1, 2, 0):
            self.copy(k).start()
        self.near(0, self.i[0].at[self.layer], self.b[0]).start()

    def put(self):
        return self.near(1, self.b[0], self.o[0].at[rows_of(self.p.block(0), self.rows)])

    def spread(self, which):
        for k in (0, 1, 4):
            self.copy(5 + 8 * which + k).start()

    def e0(self):
        self.near(0, self.i[0].at[self.layer], self.b[0]).wait()
        self.put().start()
        for which in range(2):
            self.copy(1 + which).wait_recv()
            self.copy(3 + which).start()
            self.spread(which)

    def e1(self):
        for k in (3, 4):
            self.copy(k).wait_recv()
        self.spread(2)

    def on(self, which):
        for k in range(2):
            self.copy(5 + 8 * which + k).wait_recv()
            self.copy(5 + 8 * which + 2 + k).start()
            self.copy(5 + 8 * which + 5 + k).start()

    def e2(self):
        self.on(0)
        self.on(1)

    def e3(self):
        self.on(2)

    def e4(self):
        for which in range(3):
            for k in (2, 3):
                self.copy(5 + 8 * which + k).wait_recv()
            self.copy(5 + 8 * which + 7).start()

    def e5(self):
        for k in [0] + [5 + 8 * which + j for which in range(3) for j in range(4, 8)]:
            self.copy(k).wait_recv()
        for k in range(29):
            self.copy(k).wait_send()
        self.put().wait()

    def events(self):
        return [self.e0, self.e1, self.e2, self.e3, self.e4, self.e5]


class Scatter(Comm):
    def __init__(self, g, ns, nr=None):
        self.rows, self.cols = g.shape[0] // ns, g.shape[1]
        self.pieces = 1 if nr is None else ns // 2
        self.ring = ("x+", "x-") if nr is None else ("y+", "y-")
        self.peers = ("partner",) + self.ring
        self.first = 4 * self.pieces
        self.remote, self.local = self.first + 6, self.first + 1
        self.ins, self.outs = [g], [like((self.rows, self.cols))]

    def buffers(self):
        r, c = self.rows, self.cols
        (_, a), (_, b) = halves(r)
        shapes = [(4, r, c), (4, r, c), (a, c), (b, c), (r, c), (r, c)]
        return [pltpu.VMEM(shape, BF) for shape in shapes]

    def source(self, j, piece, other):
        p, r = self.p, self.rows
        offset = (2, 1, 3, 0)[j]
        if self.pieces == 1:
            return self.i[0].at[rows_of(p.block(offset, other), r)]
        q = r // self.pieces
        core = 1 - p.c if other else p.c
        return self.i[0].at[rows_of(2 * piece + core, r, lax.rem(p.y + offset, p.nr) * q, q)]

    def into(self, ref, j, piece):
        q = self.rows // self.pieces
        return ref.at[j, pl.ds(piece * q, q)]

    def term(self, j, piece):
        return self.far(j * self.pieces + piece, self.source(j, piece, True), self.into(self.b[1], j, piece), "partner")

    def load(self, j, piece):
        return self.near(j * self.pieces + piece, self.source(j, piece, False), self.into(self.b[0], j, piece))

    def copy(self, k):
        own, ra, x1m, x1p, x2m, x2p = self.b
        (s0, n0), (s1, n1) = halves(self.rows)
        h0, h1 = pl.ds(s0, n0), pl.ds(s1, n1)
        src, dst, to = (
            (own.at[0, h0], x1m, 0),
            (own.at[0, h1], x1p, 1),
            (own.at[1, h1], x2m.at[h1], 0),
            (own.at[2, h0], x2p.at[h0], 1),
            (own.at[1, h0], x2m.at[h0], 0),
            (own.at[2, h1], x2p.at[h1], 1),
        )[k]
        return self.far(self.first + k, src, dst, self.ring[to])

    def start(self):
        for j in range(4):
            for piece in range(self.pieces):
                self.term(j, piece).start()
                self.load(j, piece).start()

    def ready(self, j):
        for piece in range(self.pieces):
            self.load(j, piece).wait()
            self.term(j, piece).wait_recv()

    def sum(self, j, half, *more):
        own, ra = self.b[0].at[j], self.b[1].at[j]
        start, size = (0, self.rows) if half is None else halves(self.rows)[half]
        add((own, start, 0), [(own, start, 0), (ra, start, 0)] + [(ref, 0, 0) for ref in more], (size, self.cols))

    def e0(self):
        self.ready(0)
        self.sum(0, 0)
        self.copy(0).start()
        self.sum(0, 1)
        self.copy(1).start()
        self.ready(1)
        self.sum(1, 1)
        self.copy(2).start()
        self.ready(2)
        self.sum(2, 0)
        self.copy(3).start()

    def e1(self):
        self.copy(0).wait_recv()
        self.sum(1, 0, self.b[2])
        self.copy(4).start()
        self.copy(1).wait_recv()
        self.sum(2, 1, self.b[3])
        self.copy(5).start()

    def e2(self):
        self.ready(3)
        for k in range(2, 6):
            self.copy(k).wait_recv()
        self.sum(3, None, self.b[4], self.b[5])
        put = self.near(self.first, self.b[0].at[3], self.o[0])
        put.start()
        for j in range(4):
            for piece in range(self.pieces):
                self.term(j, piece).wait_send()
        for k in range(6):
            self.copy(k).wait_send()
        put.wait()

    def events(self):
        return [self.e0, self.e1, self.e2]


class Finish(Comm):
    remote, local = 10, 3

    def __init__(self, block, along):
        self.rows, self.cols = block.shape
        self.by_rows = self.rows % (8 * ROWS) == 0
        self.along = along
        self.ring = (along + "+", along + "-")
        self.peers = self.ring + ("y+", "y-")
        self.ins, self.outs = [block], [like(block.shape), like((ROWS, 128), F32)]

    def buffers(self):
        full = (self.rows, self.cols)
        one = (self.rows // 4, self.cols) if self.by_rows else (self.rows, self.cols // 4)
        return [pltpu.VMEM(shape, BF) for shape in (full, full, self.window()[2], self.window()[2], one, one)] + [pltpu.VMEM((ROWS, 128), F32)]

    def window(self, fourth=0, half=0, halved=True):
        parts = 8 if halved else 4
        at = fourth * (parts // 4) + half
        if self.by_rows:
            return at * (self.rows // parts), 0, (self.rows // parts, self.cols)
        return 0, at * (self.cols // parts), (self.rows, self.cols // parts)

    def cut(self, ref, *which):
        row, col, (rows, cols) = self.window(*which)
        if self.by_rows:
            return ref.at[pl.ds(pl.multiple_of(row, ROWS), rows)]
        return ref.at[:, pl.ds(pl.multiple_of(col, 128), cols)]

    def near_by(self, offset):
        p = self.p
        return lax.rem(p.x + offset, p.nx) if self.along == "x" else lax.rem(p.y + offset, p.nr)

    def copy(self, k):
        p, block = self.p, self.i[0]
        own, res, r1m, r1p, r2m, r2p, _ = self.b
        plus, minus = self.ring
        if k < 6:
            src, dst, to = (
                (self.cut(block, self.near_by(2), 0), r1m, plus),
                (self.cut(block, self.near_by(2), 1), r1p, minus),
                (self.cut(block, self.near_by(1), 1), self.cut(r2m, 0, 1), plus),
                (self.cut(block, self.near_by(3), 0), self.cut(r2p, 0, 0), minus),
                (self.cut(own, self.near_by(1), 0), self.cut(r2m, 0, 0), plus),
                (self.cut(own, self.near_by(3), 1), self.cut(r2p, 0, 1), minus),
            )[k]
            return self.far(k, src, dst, to)
        if k < 8:
            where = self.cut(res, p.y, 0, False)
        else:
            where = self.cut(res, lax.rem(p.y + (p.nr - 1, 1)[k - 8], p.nr), k - 8)
        return self.far(k, where, where, ("y+", "y-")[k % 2])

    def start(self):
        for k in range(4):
            self.copy(k).start()
        self.near(0, self.i[0], self.b[0]).start()

    def e0(self):
        own, _, r1m, r1p = self.b[:4]
        self.near(0, self.i[0], own).wait()
        for k, (offset, half, ref) in enumerate(((1, 0, r1m), (3, 1, r1p))):
            self.copy(k).wait_recv()
            row, col, size = self.window(self.near_by(offset), half)
            add((own, row, col), [(own, row, col), (ref, 0, 0)], size)
            self.copy(4 + k).start()

    def e1(self):
        own, res, _, _, r2m, r2p, _ = self.b
        for k in range(2, 6):
            self.copy(k).wait_recv()
        row, col, size = self.window(self.near_by(0), 0, False)
        to_row, to_col, _ = self.window(self.p.y, 0, False)
        add((res, to_row, to_col), [(own, row, col), (r2m, 0, 0), (r2p, 0, 0)], size)
        self.copy(6).start()
        self.copy(7).start()

    def e2(self):
        for k in (6, 7):
            self.copy(k).wait_recv()
            self.copy(k + 2).start()

    def e3(self):
        res, squares = self.b[1], self.b[-1]
        self.copy(8).wait_recv()
        self.copy(9).wait_recv()
        self.near(1, res, self.o[0]).start()

        def one(i, total):
            g = res[pl.ds(pl.multiple_of(i * ROWS, ROWS), ROWS), :].astype(F32)
            g = g * g
            for j in range(self.cols // 128):
                total = total + g[:, 128 * j : 128 * (j + 1)]
            return total

        squares[...] = lax.fori_loop(0, self.rows // ROWS, one, jnp.zeros((ROWS, 128), F32))
        put = self.near(2, squares, self.o[1])
        put.start()
        for k in range(10):
            self.copy(k).wait_send()
        self.near(1, res, self.o[0]).wait()
        put.wait()

    def events(self):
        return [self.e0, self.e1, self.e2, self.e3]


class Total(Comm):
    def __init__(self, squares, last, ns):
        self.ns, self.last = ns, last
        self.remote, self.local = ns - 1, len(squares) + 1
        self.ins, self.outs = list(squares), [like((8, 128), F32)]
        self.peers = tuple(range(1, ns))

    def buffers(self):
        one = (ROWS, 128)
        return [pltpu.VMEM((len(self.ins),) + one, F32), pltpu.VMEM(one, F32), pltpu.VMEM((self.ns,) + one, F32), pltpu.VMEM((8, 128), F32)]

    def copy(self, k):
        return self.far(k - 1, self.b[1], self.b[2].at[self.p.s], k)

    def start(self):
        for j, ref in enumerate(self.i):
            self.near(j, ref, self.b[0].at[j]).start()

    def e0(self):
        loaded, mine, slots, out = self.b
        total = self.last[0].b[-1][...]
        for comm in self.last[1:]:
            total = total + comm.b[-1][...]
        for j, ref in enumerate(self.i):
            self.near(j, ref, loaded.at[j]).wait()
            total = total + loaded[j]
        mine[...] = total
        for k in range(1, self.ns):
            self.copy(k).start()
        slots[self.p.s] = total
        for k in range(1, self.ns):
            self.copy(k).wait_recv()
        total = slots[0]
        for k in range(1, self.ns):
            total = total + slots[k]
        out[...] = jnp.full((8, 128), jnp.sum(total), F32)
        put = self.near(len(self.i), out, self.o[0])
        put.start()
        for k in range(1, self.ns):
            self.copy(k).wait_send()
        put.wait()

    def events(self):
        return [self.e0]


def kernel(numbers, sizes, name, compute=None, steps=1, ins=(), outs=(), resident=(), comms=(), plan=(), due=None):
    order = []
    for which, (comm, steps_of) in enumerate(zip(comms, plan, strict=True)):
        events = comm.events()
        if len(steps_of) > len(events):
            events = [comm.start] + events
            comm.late = True
        order += [(at, max(j - comm.late, 0), which, event) for j, (at, event) in enumerate(zip(steps_of, events, strict=True))]
    order.sort(key=lambda entry: entry[:-1])
    ns, nr = sizes
    peers = tuple(dict.fromkeys(peer for comm in comms for peer in comm.peers))

    def body(*refs):
        refs = list(refs)

        def take(count):
            taken = refs[:count]
            del refs[:count]
            return taken

        my_ins, my_res = take(len(ins)), take(len(resident))
        comm_ins = [take(len(comm.ins)) for comm in comms]
        my_outs = take(len(outs))
        comm_outs = [take(len(comm.outs)) for comm in comms]
        held = take(len(resident))
        sems = take(1)[0] if resident else None
        place = Place(ns, nr)
        for comm, i, o in zip(comms, comm_ins, comm_outs, strict=True):
            comm.bind(place, i, o, take(len(comm.scratch())))
        i = pl.program_id(0)
        loads = [pltpu.make_async_copy(src, dst, sems.at[j]) for j, (src, dst) in enumerate(zip(my_res, held, strict=True))]

        @pl.when(i == 0)
        def _():
            for load in loads:
                load.start()
            if peers:
                barrier = pltpu.get_barrier_semaphore()
                for peer in peers:
                    pl.semaphore_signal(barrier, inc=1, device_id=place.to(peer), device_id_type=MESH)
                pl.semaphore_wait(barrier, len(peers))
            for comm in comms:
                if not comm.late:
                    comm.start()

        for load, step in zip(loads, due or [0] * len(loads), strict=True):
            pl.when(i == step)(load.wait)

        def run(now):
            for at, _, _, event in order:
                if now(at):
                    event()

        for step in sorted({at for at, *_ in order if at < steps}):
            pl.when(i == step)(lambda step=step: run(lambda at: at == step))
        if compute is not None:
            compute(i, held, my_ins, my_outs)
        if order:
            pl.when(i == steps - 1)(lambda: run(lambda at: at >= steps))

    scratch = [pltpu.VMEM(a.shape, a.dtype) for a in resident]
    if resident:
        scratch.append(pltpu.SemaphoreType.DMA((len(resident),)))
    for comm in comms:
        scratch += comm.scratch()
    results = pl.pallas_call(
        body,
        grid=(steps,),
        in_specs=[spec for _, spec in ins] + [ANY] * (len(resident) + sum(len(comm.ins) for comm in comms)),
        out_specs=[spec for _, spec in outs] + [ANY] * sum(len(comm.outs) for comm in comms),
        out_shape=[shape for shape, _ in outs] + [shape for comm in comms for shape in comm.outs],
        scratch_shapes=scratch,
        name=name,
        compiler_params=pltpu.CompilerParams(
            vmem_limit_bytes=62 << 20,
            dimension_semantics=("arbitrary",),
            **({"collective_id": next(numbers), "has_side_effects": True} if comms else {}),
        ),
    )(*[a for a, _ in ins], *resident, *[a for comm in comms for a in comm.ins])
    results = list(results)
    mine, rest = results[: len(outs)], results[len(outs) :]
    theirs = []
    for comm in comms:
        theirs.append(rest[: len(comm.outs)])
        rest = rest[len(comm.outs) :]
    return mine, theirs


def rows_spec(size, cols):
    return pl.BlockSpec((size, cols), lambda i: (i, 0))


def cols_spec(rows, size):
    return pl.BlockSpec((rows, size), lambda i: (0, i))


def whole(function):
    def compute(i, held, ins, outs):
        for out, value in zip(outs, function(*[ref[...] for ref in (*ins, *held)]), strict=True):
            out[...] = value

    return compute


def normed(wide):
    scale = lax.rsqrt(jnp.mean(wide * wide, -1, keepdims=True) + 1e-6)
    return (wide * scale).astype(BF), scale


def adamw(w, m, v, g):
    m = 0.9 * m + 0.1 * g
    v = 0.95 * v + 0.05 * g * g
    step = m * lax.rsqrt(v + 1e-8) + 0.1 * w
    return (w - 0.02 * step).astype(BF), m, v


def solution(mesh):
    sizes = ns, nr = mesh.shape["s"], mesh.shape["r"]

    def step(x, dy, *arrays):
        weights, m, v = (arrays[i : i + 3] for i in (0, 3, 6))
        w_gate, w_up, w_down = weights
        x, dy = x[0], dy[0]
        tokens, d = x.shape
        ff = w_gate.shape[2]
        tile = 256
        n = tokens // tile
        call = functools.partial(kernel, itertools.count(), sizes)
        thin, wide = rows_spec(tile, d), rows_spec(tile, ff)

        def matrices(layer):
            return [GatherAcross(w_gate, layer, ns, nr), GatherAcross(w_up, layer, ns, nr), Gather(w_down, layer, ns)]

        early, last = range(1, 7), (3, 4, 6, 7)
        _, ((wg0,), (wu0,), (wd0,)) = call("first", comms=matrices(0), plan=(early, early, (1, *range(4, 7))))

        @whole
        def forward(h, w_gate, w_up, w_down):
            a, _ = normed(h.astype(F32))
            gate, up = dot(a, w_gate), dot(a, w_up)
            sig = jax.nn.sigmoid(gate)
            silu = gate * sig
            act = (silu * up).astype(BF)
            h = h + dot(act, w_down).astype(BF)
            return a, up * slope(gate, sig), silu, act, h, normed(h.astype(F32))[0]

        def slope(gate, sig):
            return sig * (1.0 + gate * (1.0 - sig))

        narrow, broad, exact = (like((tokens, d)), thin), (like((tokens, ff)), wide), (like((tokens, ff), F32), wide)
        (a0, slope0, silu0, act0, h1, a1), ((wg1,), (wu1,), (wd1,)) = call(
            "forward", forward, n, [(x, thin)], [narrow, exact, exact, broad, narrow, narrow],
            (wg0, wu0, wd0), matrices(1), ((1, 2, 3, 5, 7, n), (1, 2, 4, 5, 7, n), (1, 5, 7, n)),
        )

        @whole
        def turn(a, dy, w_gate, w_up, w_down):
            dact = dot(dy, w_down, NT).astype(BF).astype(F32)
            gate, up = dot(a, w_gate), dot(a, w_up)
            sig = jax.nn.sigmoid(gate)
            silu = gate * sig
            return (silu * up).astype(BF), (dact * (up * slope(gate, sig))).astype(BF), (dact * silu).astype(BF)

        (act1, dgate1, dup1), _ = call("turn", turn, n, [(a1, thin), (dy, thin)], [broad] * 3, (wg1, wu1, wd1))

        @whole
        def product(act, dh):
            return (dot(act, dh, TN).astype(BF),)

        def by_down(act, dh, comms=(), plan=()):
            size = 5 * 128
            return call(
                "by_down", product, ff // size, [(act, cols_spec(tokens, size))],
                [(like((ff, d)), rows_spec(size, d))], (dh,), comms, plan,
            )

        def by_both(a, dgate, dup, comms, plan):
            size = 128
            k = d // size

            def products(i, held, ins, outs):
                for which, now in enumerate((i < k, i >= k)):
                    part = slice(which, which + 1)
                    pl.when(now)(lambda part=part: product(i, held[part], ins, outs[part]))

            return call(
                "by_both", products, 2 * k, [(a, pl.BlockSpec((tokens, size), lambda i: (0, lax.rem(i, k))))],
                [
                    (like((d, ff)), pl.BlockSpec((size, ff), lambda i: (jnp.minimum(i, k - 1), 0))),
                    (like((d, ff)), pl.BlockSpec((size, ff), lambda i: (jnp.maximum(i - k, 0), 0))),
                ],
                (dgate, dup), comms, plan, (0, k),
            )

        (gd1,), _ = by_down(act1, dy)
        (gg1, gu1), ((sd1,),) = by_both(a1, dgate1, dup1, [Scatter(gd1, ns)], [(2, 7, 14)])

        @whole
        def by_states(dgate, dup, h, dy, w_gate, w_up):
            da = (dot(dgate, w_gate, NT).astype(BF) + dot(dup, w_up, NT).astype(BF)).astype(F32)
            h = h.astype(F32)
            _, scale = normed(h)
            dh = da * scale - h * (scale * scale * scale * jnp.mean(da * h, -1, keepdims=True))
            return (dy + dh.astype(BF),)

        (dh1,), ((sg1,), (su1,)) = call(
            "by_states", by_states, n, [(dgate1, wide), (dup1, wide), (h1, thin), (dy, thin)], [narrow],
            (wg1, wu1), [Scatter(gg1, ns), Scatter(gu1, ns, nr)], [(1, 4, n)] * 2,
        )

        @whole
        def by_act(dh, slope, silu, w_down):
            dact = dot(dh, w_down, NT).astype(BF).astype(F32)
            return (dact * slope).astype(BF), (dact * silu).astype(BF)

        (dgate0, dup0), ((rd1, qd1),) = call(
            "by_act", by_act, n, [(dh1, thin), (slope0, wide), (silu0, wide)], [broad] * 2,
            (wd0,), [Finish(sd1, "y")], [last],
        )
        (gd0,), ((rg1, qg1),) = by_down(act0, dh1, [Finish(sg1, "y")], [(1, 2, 4, 5)])
        (gg0, gu0), ((sd0,), (ru1, qu1)) = by_both(a0, dgate0, dup0, [Scatter(gd0, ns), Finish(su1, "x")], [(3, 8, 15), (2, 4, 6, 9)])
        _, ((sg0,), (rd0, qd0), (su0,)) = call(
            "tail", comms=[Scatter(gg0, ns), Finish(sd0, "y"), Scatter(gu0, ns, nr)], plan=[(1, 4, 6), (2, 3, 3, 5), (2, 4, 6)]
        )
        finish = [Finish(sg0, "y"), Finish(su0, "x")]
        _, ((rg0, _), (ru0, _), (total,)) = call("last", comms=finish + [Total([qd1, qg1, qu1, qd0], finish, ns)], plan=[last, last, [n]])

        gradients = [jnp.stack(pair).astype(F32) for pair in ((rg0, rg1), (ru0, ru1), (rd0, rd1))]
        count = ns * sum(g.size for g in gradients)
        factor = jnp.minimum(1.0, 0.5 * lax.rsqrt(total[0, 0] / count + 1e-30))
        new = [adamw(w.astype(F32), m, v, g * factor) for w, m, v, g in zip(weights, m, v, gradients, strict=True)]
        return tuple(one[which] for which in range(len(weights)) for one in new)

    states, cut = P(("rep", "r", "s")), P(None, "s")
    return jax.shard_map(
        step,
        mesh=mesh,
        in_specs=(states, states) + (cut,) * 9,
        out_specs=(P("rep", "s"),) * 9,
        check_vma=False,
    )
```

time: 789 us -> 524 us (0.66)
  the two profiles are of different devices: /device:TPU:96 before, /device:TPU:97 now
where the time goes in v1:
time: 524 us; the launch traced here: 514 us
  Pallas kernels  491 us (94%)
  other arithmetic  16.2 us (3%)
    pallas_call x11, Pallas kernels, kernel(): pl.pallas_call(body, grid=(steps,), in_specs=[spec for _, spec in ins] +...  491 us
    convert_element_type x2, other arithmetic, adamw(): return ((w - 0.02 * step).astype(BF), m, v)  16.2 us

profile of v1, /device:TPU:97, one launch (start us, length us, event | category | flops | bytes accessed | tf_op | source)
XLA Modules:
  0.0 513.9 jit_solution(14027046322415126978)
XLA Ops:
  0.6 56.9 %first.1 = (bf16[1024,3200]{1,0:T(8,128)(2,1)}, bf16[1024,3200]{1,0:T(8,128)(2,1)}, bf16[3200,1024]{1,0:T(8,128)(2,1)}) custom-call(bf16[2,128,3200]{2,1,0:T(8,128)(2,1)} %refs_4_.1, bf16[2,128,3200]{2,1,0:T(8,128)(2,1)} %refs_5_.1, bf16[2,400,1024]{2,1,0:T(8,128)(2,1)} %refs_6_.1), custom_call_target="tpu_custom_call" | custom-call | tf_op jit(solution)/shard_map/first/pallas_call | solution.py:579
  57.5 68.0 %forward.1 = (bf16[2048,1024]{1,0:T(8,128)(2,1)}, f32[2048,3200]{1,0:T(8,128)}, f32[2048,3200]{1,0:T(8,128)}, bf16[2048,3200]{1,0:T(8,128)(2,1)}, bf16[2048,1024...) custom-call(bf16[2048,1024]{1,0:T(8,128)(2,1)} %bitcast.12, ...), custom_call_target="tpu_custom_call" | custom-call | tf_op jit(solution)/shard_map/forward/pallas_call | solution.py:579
  125.5 57.9 %turn.1 = (bf16[2048,3200]{1,0:T(8,128)(2,1)}, bf16[2048,3200]{1,0:T(8,128)(2,1)}, bf16[2048,3200]{1,0:T(8,128)(2,1)}) custom-call(bf16[2048,1024]{1,0:T(8,128)(2,1)} %get-tuple-element.53.refs_0_, bf16[2048,1024]{1,0:T(8,128)(2,1)} %bitcast.9, bf16[1024,3200]{1,0:T(8,128)(2,1)} %get-tuple-element.54.refs_2_.refs_4_, ...), custom_call_target="tpu_custom_call" | custom-call | tf_op jit(solution)/shard_map/turn/pallas_call | solution.py:579
  183.4 19.7 %by_down.2.refs_3_ = bf16[3200,1024]{1,0:T(8,128)(2,1)} custom-call(bf16[2048,3200]{1,0:T(8,128)(2,1)} %get-tuple-element.60.refs_0_, bf16[2048,1024]{1,0:T(8,128)(2,1)} %bitcast.10), custom_call_target="tpu_custom_call" | custom-call | tf_op jit(solution)/shard_map/by_down/pallas_call | solution.py:579
  203.2 45.5 %by_both.2 = (bf16[1024,3200]{1,0:T(8,128)(2,1)}, bf16[1024,3200]{1,0:T(8,128)(2,1)}, bf16[400,1024]{1,0:T(8,128)(2,1)}) custom-call(bf16[2048,1024]{1,0:T(8,128)(2,1)} %get-tuple-element.53.refs_0_, bf16[2048,3200]{1,0:T(8,128)(2,1)} %get-tuple-element.57.refs_1_.refs_0_, bf16[2048,3200]{1,0:T(8,128)(2,1)} %get-tuple-element.58.refs_2_.refs_1_, ...), custom_call_target="tpu_custom_call" | custom-call | tf_op jit(solution)/shard_map/by_both/pallas_call | solution.py:579
  248.7 47.4 %by_states.1 = (bf16[2048,1024]{1,0:T(8,128)(2,1)}, bf16[128,3200]{1,0:T(8,128)(2,1)}, bf16[128,3200]{1,0:T(8,128)(2,1)}) custom-call(bf16[2048,3200]{1,0:T(8,128)(2,1)} %get-tuple-element.57.refs_1_.refs_0_, bf16[2048,3200]{1,0:T(8,128)(2,1)} %get-tuple-element.58.refs_2_.refs_1_, bf16[2048,1024]{1,0:T(8,128)(2,1)} %get-tuple-element.59.refs_2_, ...), custom_call_target="tpu_custom_call" | custom-call | tf_op jit(solution)/shard_map/by_states/pallas_call | solution.py:579
  296.1 39.5 %by_act.1 = (bf16[2048,3200]{1,0:T(8,128)(2,1)}, bf16[2048,3200]{1,0:T(8,128)(2,1)}, bf16[400,1024]{1,0:T(8,128)(2,1)}, f32[16,128]{1,0:T(8,128)}) custom-call(bf16[2048,1024]{1,0:T(8,128)(2,1)} %get-tuple-element.63.refs_0_.refs_1_, f32[2048,3200]{1,0:T(8,128)} %get-tuple-element.64.refs_1_, f32[2048,3200]{1,0:T(8,128)} %get-tuple-element.65.refs_2_, ...), custom_call_target="tpu_custom_call" | custom-call | tf_op jit(solution)/shard_map/by_act/pallas_call | solution.py:579
  335.6 22.9 %by_down.3 = (bf16[3200,1024]{1,0:T(8,128)(2,1)}, bf16[128,3200]{1,0:T(8,128)(2,1)}, f32[16,128]{1,0:T(8,128)}) custom-call(bf16[2048,3200]{1,0:T(8,128)(2,1)} %get-tuple-element.69.refs_0_, bf16[2048,1024]{1,0:T(8,128)(2,1)} %get-tuple-element.63.refs_0_.refs_1_, bf16[128,3200]{1,0:T(8,128)(2,1)} %get-tuple-element.70.refs_2_), custom_call_target="tpu_custom_call" | custom-call | tf_op jit(solution)/shard_map/by_down/pallas_call | solution.py:579
  358.5 47.5 %by_both.3 = (bf16[1024,3200]{1,0:T(8,128)(2,1)}, bf16[1024,3200]{1,0:T(8,128)(2,1)}, bf16[400,1024]{1,0:T(8,128)(2,1)}, bf16[128,3200]{1,0:T(8,128)(2,1)}, f32[16,128]{1,0:T(8,128)}) custom-call(bf16[2048,1024]{1,0:T(8,128)(2,1)} %get-tuple-element.52.refs_0_, bf16[2048,3200]{1,0:T(8,128)(2,1)} %get-tuple-element.67.refs_1_, ...), custom_call_target="tpu_custom_call" | custom-call | tf_op jit(solution)/shard_map/by_both/pallas_call | solution.py:579
  406.0 0.0 copy-start
  406.0 52.2 %tail.1 = (bf16[128,3200]{1,0:T(8,128)(2,1)}, bf16[400,1024]{1,0:T(8,128)(2,1)}, f32[16,128]{1,0:T(8,128)}, bf16[128,3200]{1,0:T(8,128)(2,1)}) custom-call(bf16[1024,3200]{1,0:T(8,128)(2,1)} %get-tuple-element.73.refs_0_, bf16[400,1024]{1,0:T(8,128)(2,1)} %get-tuple-element.74.refs_1_, bf16[1024,3200]{1,0:T(8,128)(2,1)} %get-tuple-element.75.refs_2_), custom_call_target="tpu_custom_call" | custom-call | tf_op jit(solution)/shard_map/tail/pallas_call | solution.py:579
  458.3 33.1 %last.1 = (bf16[128,3200]{1,0:T(8,128)(2,1)}, f32[16,128]{1,0:T(8,128)}, bf16[128,3200]{1,0:T(8,128)(2,1)}, f32[16,128]{1,0:T(8,128)}, f32[8,128]{1,0:T(8,128)}) custom-call(bf16[128,3200]{1,0:T(8,128)(2,1)} %get-tuple-element.76.refs_0_, bf16[128,3200]{1,0:T(8,128)(2,1)} %get-tuple-element.77.refs_1_, f32[16,128]{1,0:T(8,128)} %get-tuple-element.78.refs_2_, ...), custom_call_target="tpu_custom_call" | custom-call | tf_op jit(solution)/shard_map/last/pallas_call | solution.py:579
  491.4 1.2 slice.3
  493.3 0.0 copy-start.1
  493.3 0.0 copy-start.2
  493.3 0.0 copy-start.5
  493.3 7.4 %fusion.8 = (bf16[2,400,1024]{2,1,0:T(8,128)(2,1)}, f32[2,400,1024]{2,1,0:T(8,128)}, f32[2,400,1024]{2,1,0:T(8,128)}) fusion(bf16[2,400,1024]{2,1,0:T(8,128)(2,1)S(1)} %copy-done, f32[]{:T(128)} %bitcast.4, bf16[1,400,1024]{2,1,0:T(8,128)(2,1)} %bitcast.17, bf16[1,400,1024]{2,1,0:T(8,128)(2,1)} %bitcast.18, f32[2,400,1024]{2,1,0:T(8,128)} %param.21, ...), kind=kLoop, calls=%fused_computation.17 | loop fusion | flops 16384000 | bytes 18022404 | tf_op jit(solution)/shard_map/convert_element_type | solution.py:627
  500.8 0.1 copy-done.3
  500.9 1.6 copy-done.4
  502.4 0.9 copy-done.5
  503.4 0.9 copy-done.6
  504.3 0.1 copy-done.7
  504.4 0.2 copy-done.8
  504.7 8.8 %fusion.2 = (bf16[2,128,3200]{2,1,0:T(8,128)(2,1)}, f32[2,128,3200]{2,1,0:T(8,128)}, f32[2,128,3200]{2,1,0:T(8,128)}, bf16[2,128,3200]{2,1,0:T(8,128)(2,1)}, f32...) fusion(bf16[2,128,3200]{2,1,0:T(8,128)(2,1)S(1)} %copy-done.1, f32[]{:T(128)} %bitcast.4, ...), kind=kLoop, calls=%fused_computation.11 | loop fusion | flops 32768000 | bytes 36044804 | tf_op jit(solution)/shard_map/convert_element_type | solution.py:627
  (8 shorter events, 0.0 us)
Async XLA Ops:
  406.0 87.2 %copy-start = (bf16[2,400,1024]{2,1,0:T(8,128)(2,1)S(1)}, bf16[2,400,1024]{2,1,0:T(8,128)(2,1)}, u32[]{:S(2)}) copy-start(bf16[2,400,1024]{2,1,0:T(8,128)(2,1)} %refs_6_.1) | copy-start | bytes 4915204
  493.3 7.5 %copy-start.1 = (bf16[2,128,3200]{2,1,0:T(8,128)(2,1)S(1)}, bf16[2,128,3200]{2,1,0:T(8,128)(2,1)}, u32[]{:S(2)}) copy-start(bf16[2,128,3200]{2,1,0:T(8,128)(2,1)} %refs_4_.1) | copy-start | bytes 4915204
  493.3 7.5 %copy-start.2 = (bf16[2,128,3200]{2,1,0:T(8,128)(2,1)S(1)}, bf16[2,128,3200]{2,1,0:T(8,128)(2,1)}, u32[]{:S(2)}) copy-start(bf16[2,128,3200]{2,1,0:T(8,128)(2,1)} %refs_5_.1) | copy-start | bytes 4915204
  493.3 7.6 %copy-start.3 = (f32[2,128,3200]{2,1,0:T(8,128)S(1)}, f32[2,128,3200]{2,1,0:T(8,128)}, u32[]{:S(2)}) copy-start(f32[2,128,3200]{2,1,0:T(8,128)} %param.19) | copy-start | bytes 9830404
  493.3 9.1 %copy-start.4 = (f32[2,128,3200]{2,1,0:T(8,128)S(1)}, f32[2,128,3200]{2,1,0:T(8,128)}, u32[]{:S(2)}) copy-start(f32[2,128,3200]{2,1,0:T(8,128)} %param.16) | copy-start | bytes 9830404
  493.3 10.1 %copy-start.5 = (f32[2,128,3200]{2,1,0:T(8,128)S(1)}, f32[2,128,3200]{2,1,0:T(8,128)}, u32[]{:S(2)}) copy-start(f32[2,128,3200]{2,1,0:T(8,128)} %param.20) | copy-start | bytes 9830404
  493.3 11.0 %copy-start.6 = (f32[2,128,3200]{2,1,0:T(8,128)S(1)}, f32[2,128,3200]{2,1,0:T(8,128)}, u32[]{:S(2)}) copy-start(f32[2,128,3200]{2,1,0:T(8,128)} %param.17) | copy-start | bytes 9830404
  493.3 11.1 %copy-start.7 = (bf16[128,3200]{1,0:T(8,128)(2,1)S(1)}, bf16[128,3200]{1,0:T(8,128)(2,1)}, u32[]{:S(2)}) copy-start(bf16[128,3200]{1,0:T(8,128)(2,1)} %get-tuple-element.83) | copy-start | bytes 2457604
  493.3 11.3 %copy-start.8 = (bf16[128,3200]{1,0:T(8,128)(2,1)S(1)}, bf16[128,3200]{1,0:T(8,128)(2,1)}, u32[]{:S(2)}) copy-start(bf16[128,3200]{1,0:T(8,128)(2,1)} %get-tuple-element.86) | copy-start | bytes 2457604
